TPU v7x, 32 devices: a whole 2x2x4 slice. The times are simulated.
32 devices in a mesh: wide: 8 (over z, x), narrow: 4 (over y, core).
Axes of the slice: x: 2, y: 2, z: 4, core: 2. Of those that a mesh axis runs over, the one named last changes fastest.
Arguments:
- tokens: bfloat16 [3, 10240, 768], P(None, 'wide'), may hold values from -6 to 6
- image_lengths: int32 [3, 8, 8], P(None, 'wide'), may hold values from 1 to 196, 1280 in all within a row
- heads_weight: bfloat16 [768, 3, 768], P('wide', None, 'narrow'), may hold values from -0.21875 to 0.21875
- heads_bias: float32 [2, 768], P(None, 'narrow'), may hold values from -3 to 3
- out_weight: bfloat16 [768, 768], P('narrow', 'wide'), may hold values from -1.75 to 1.75
- out_bias: float32 [768], replicated, may hold values from -3 to 3
- up_weight: bfloat16 [768, 3072], P('wide', 'narrow'), may hold values from -0.21875 to 0.21875
- up_bias: float32 [3072], P('narrow'), may hold values from -3 to 3
- down_weight: bfloat16 [3072, 768], P('narrow', 'wide'), may hold values from -0.109375 to 0.109375
- down_bias: float32 [768], replicated, may hold values from -3 to 3
- first_gain: float32 [768], replicated, may hold values from 0.1 to 1.9
- first_shift: float32 [768], replicated, may hold values from -3 to 3
- second_gain: float32 [768], replicated, may hold values from 0.1 to 1.9
- second_shift: float32 [768], replicated, may hold values from -3 to 3
- mixer_scale: float32 [768], replicated, may hold values from 0.5 to 2
- feed_scale: float32 [768], replicated, may hold values from 0.5 to 2
- cotangent: bfloat16 [3, 10240, 768], P(None, 'wide'), may hold values from -6 to 6
Outputs:
- layer_out: bfloat16 [3, 10240, 768], P(None, 'wide')
- token_grad: bfloat16 [3, 10240, 768], P(None, ('wide', 'narrow'))
- heads_weight_grad: float32 [768, 3, 768], P(None, None, 'narrow')
- heads_bias_grad: float32 [2, 768], P(None, 'narrow')
- out_weight_grad: float32 [768, 768], P('narrow')
- out_bias_grad: float32 [768], replicated
- up_weight_grad: float32 [768, 3072], P(None, 'narrow')
- up_bias_grad: float32 [3072], P('narrow')
- down_weight_grad: float32 [3072, 768], P('narrow')
- down_bias_grad: float32 [768], replicated
- first_gain_grad: float32 [768], replicated
- first_shift_grad: float32 [768], replicated
- second_gain_grad: float32 [768], replicated
- second_shift_grad: float32 [768], replicated
- mixer_scale_grad: float32 [768], replicated
- feed_scale_grad: float32 [768], replicated
Inputs may be any that keep to these rules, and one draw needn't show every extreme that they name: `image_lengths`: each row of 8 numbers gives the lengths of the images packed in order into one micro-batch of one index of wide; they sum to 1280, and the largest is 196.
All inputs are finite; a program needn't handle non-finite values.
Results may differ from a plain program's by a relative error of at most 0.02.
Values may be sent and summed in bfloat16 or wider, within the bound.
No kernel may reach another device: no remote copies, remote signals or barrier semaphores. Data moves between devices by JAX's collectives and lax.ppermute only.
A program may use at most 256 MiB of HBM per device.

v0:
```python
from functools import partial
from functools import reduce
import jax
import jax.numpy as jnp
from jax import lax
from jax.sharding import PartitionSpec as P

HEAD_DIM = 64
QUERY_BLOCK = 640
epsilon = 1e-06


def norm_parts(values_in):
    center = jnp.mean(values_in, axis=-1, keepdims=True)
    shifted = values_in - center
    inverse = lax.rsqrt(jnp.mean(shifted * shifted, axis=-1, keepdims=True) + epsilon)
    return (shifted * inverse, inverse)


def norm_back(grad_in, unit_rows, inverse, gain_row):
    scaled = grad_in * gain_row
    return inverse * (
        scaled
        - jnp.mean(scaled, axis=-1, keepdims=True)
        - unit_rows * jnp.mean(scaled * unit_rows, axis=-1, keepdims=True)
    )


def image_index(sizes_row, row_count):
    bounds = jnp.cumsum(sizes_row)
    places = jnp.arange(row_count, dtype=jnp.int32)
    return jnp.sum((places[:, None] >= bounds[None, :]).astype(jnp.int32), axis=1)


def exact_gelu(values_in):
    return jax.nn.gelu(values_in, approximate=False)


def attend_forward(key_heads, value_heads, attention_scale, block_items):
    query_heads, same_image = block_items
    raw_scores = (
        jnp.einsum("qhc,khc->hqk", query_heads, key_heads, preferred_element_type=jnp.float32)
        * attention_scale
    )
    scores = jnp.where(same_image[None], raw_scores, -1e30)
    row_max = jnp.max(scores, axis=-1, keepdims=True)
    exp_scores = jnp.exp(scores - row_max)
    exp_total = jnp.sum(exp_scores, axis=-1, keepdims=True)
    soft_weights = (exp_scores / exp_total).astype(jnp.bfloat16)
    context = jnp.einsum(
        "hqk,khc->qhc", soft_weights, value_heads, preferred_element_type=jnp.float32
    )
    return (context, row_max + jnp.log(exp_total))


def attend_back(key_heads, value_heads, attention_scale, running, block_items):
    query_heads, context_grad, same_image, log_total = block_items
    raw_scores = (
        jnp.einsum("qhc,khc->hqk", query_heads, key_heads, preferred_element_type=jnp.float32)
        * attention_scale
    )
    scores = jnp.where(same_image[None], raw_scores, -1e30)
    soft_weights = jnp.exp(scores - log_total)
    weight_grad = jnp.einsum(
        "qhc,khc->hqk", context_grad, value_heads, preferred_element_type=jnp.float32
    )
    row_delta = jnp.sum(soft_weights * weight_grad, axis=-1, keepdims=True)
    score_grad = (soft_weights * (weight_grad - row_delta)).astype(jnp.bfloat16)
    query_grad = (
        jnp.einsum("hqk,khc->qhc", score_grad, key_heads, preferred_element_type=jnp.float32)
        * attention_scale
    )
    key_grad = (
        jnp.einsum("hqk,qhc->khc", score_grad, query_heads, preferred_element_type=jnp.float32)
        * attention_scale
    )
    value_grad = jnp.einsum(
        "hqk,qhc->khc",
        soft_weights.astype(jnp.bfloat16),
        context_grad,
        preferred_element_type=jnp.float32,
    )
    return ((running[0] + key_grad, running[1] + value_grad), query_grad)


def feed_term(upper_grad, up_full):
    return jnp.einsum("rf,df->rd", upper_grad, up_full, preferred_element_type=jnp.float32)


def heads_term_rows(heads_grad, heads_full):
    return jnp.einsum("rtc,dtc->rd", heads_grad, heads_full, preferred_element_type=jnp.float32)


def add_tuples(left, right):
    return jax.tree.map(jnp.add, left, right)


def body(
    tokens,
    image_lengths,
    heads_weight,
    heads_bias,
    out_weight,
    out_bias,
    up_weight,
    up_bias,
    down_weight,
    down_bias,
    first_gain,
    first_shift,
    second_gain,
    second_shift,
    mixer_scale,
    feed_scale,
    cotangent,
):
    micro_count, row_count, width = tokens.shape
    quarter = row_count // lax.axis_size("narrow")
    quarter_start = lax.axis_index("narrow") * quarter
    attention_scale = HEAD_DIM ** (-0.5)
    head_local = heads_weight.shape[2] // HEAD_DIM
    block_count = row_count // QUERY_BLOCK

    def quarter_rows(values_in):
        return lax.dynamic_slice_in_dim(values_in, quarter_start, quarter, 0)

    zero_row = jnp.zeros((width,), jnp.float32)
    out_bias_sum, down_bias_sum = (zero_row, zero_row)
    first_gain_sum, first_shift_sum = (zero_row, zero_row)
    second_gain_sum, second_shift_sum = (zero_row, zero_row)
    mixer_scale_sum, feed_scale_sum = (zero_row, zero_row)
    head_bias_sum = jnp.zeros(heads_bias.shape, jnp.float32)
    up_bias_sum = jnp.zeros(up_bias.shape, jnp.float32)
    term_list = []
    outputs = []
    input_grads = []
    for micro_index in range(micro_count):
        gathered = (
            lax.all_gather(heads_weight, "wide", axis=0, tiled=True),
            lax.all_gather(out_weight, "wide", axis=1, tiled=True),
            lax.all_gather(up_weight, "wide", axis=0, tiled=True),
            lax.all_gather(down_weight, "wide", axis=1, tiled=True),
        )
        heads_full, out_full, up_full, down_full = gathered
        token_rows = tokens[micro_index].astype(jnp.float32)
        index_row = image_index(image_lengths[micro_index, 0], row_count)
        same_image = index_row[:, None] == index_row[None, :]
        first_unit, first_inverse = norm_parts(token_rows)
        first_normed = (first_unit * first_gain + first_shift).astype(jnp.bfloat16)
        projected = jnp.einsum(
            "rd,dtc->rtc", first_normed, heads_full, preferred_element_type=jnp.float32
        )
        query_heads = (
            (projected[:, 0] + heads_bias[0])
            .astype(jnp.bfloat16)
            .reshape(row_count, head_local, HEAD_DIM)
        )
        key_heads = projected[:, 1].astype(jnp.bfloat16).reshape(row_count, head_local, HEAD_DIM)
        value_heads = (
            (projected[:, 2] + heads_bias[1])
            .astype(jnp.bfloat16)
            .reshape(row_count, head_local, HEAD_DIM)
        )
        query_blocks = query_heads.reshape(block_count, QUERY_BLOCK, head_local, HEAD_DIM)
        same_blocks = same_image.reshape(block_count, QUERY_BLOCK, row_count)
        context_blocks, log_total = lax.map(
            partial(attend_forward, key_heads, value_heads, attention_scale),
            (query_blocks, same_blocks),
        )
        context = context_blocks.reshape(row_count, head_local * HEAD_DIM).astype(jnp.bfloat16)
        mixed = lax.psum(
            jnp.dot(context, out_full, preferred_element_type=jnp.float32).astype(jnp.bfloat16),
            "narrow",
        ).astype(jnp.float32)
        middle = token_rows + mixer_scale * (mixed + out_bias)
        second_unit, second_inverse = norm_parts(middle)
        second_normed = (second_unit * second_gain + second_shift).astype(jnp.bfloat16)
        upper = jnp.dot(second_normed, up_full, preferred_element_type=jnp.float32) + up_bias
        active, gelu_slope = jax.vjp(exact_gelu, upper)
        active = active.astype(jnp.bfloat16)
        feed = lax.psum(
            jnp.dot(active, down_full, preferred_element_type=jnp.float32).astype(jnp.bfloat16),
            "narrow",
        ).astype(jnp.float32)
        outputs.append((middle + feed_scale * (feed + down_bias)).astype(jnp.bfloat16))
        output_grad = cotangent[micro_index].astype(jnp.float32)
        feed_grad = (feed_scale * output_grad).astype(jnp.bfloat16)
        active_grad = jnp.einsum(
            "rd,fd->rf", feed_grad, down_full, preferred_element_type=jnp.float32
        )
        down_term = jnp.einsum("rf,rd->fd", active, feed_grad, preferred_element_type=jnp.float32)
        upper_grad = gelu_slope(active_grad)[0].astype(jnp.bfloat16)
        up_term = jnp.einsum(
            "rd,rf->df", second_normed, upper_grad, preferred_element_type=jnp.float32
        )
        up_bias_sum = up_bias_sum + jnp.sum(upper_grad.astype(jnp.float32), axis=0)
        second_normed_grad = lax.psum_scatter(
            feed_term(upper_grad, up_full).astype(jnp.bfloat16),
            "narrow",
            scatter_dimension=0,
            tiled=True,
        ).astype(jnp.float32)
        out_quarter = quarter_rows(output_grad)
        second_unit_part = quarter_rows(second_unit)
        second_gain_sum = second_gain_sum + jnp.sum(second_normed_grad * second_unit_part, axis=0)
        second_shift_sum = second_shift_sum + jnp.sum(second_normed_grad, axis=0)
        feed_scale_sum = feed_scale_sum + jnp.sum(
            out_quarter * (quarter_rows(feed) + down_bias), axis=0
        )
        down_bias_sum = down_bias_sum + feed_scale * jnp.sum(out_quarter, axis=0)
        middle_grad = out_quarter + norm_back(
            second_normed_grad, second_unit_part, quarter_rows(second_inverse), second_gain
        )
        mixer_scale_sum = mixer_scale_sum + jnp.sum(
            middle_grad * (quarter_rows(mixed) + out_bias), axis=0
        )
        out_bias_sum = out_bias_sum + mixer_scale * jnp.sum(middle_grad, axis=0)
        mixed_grad = lax.all_gather(
            (mixer_scale * middle_grad).astype(jnp.bfloat16), "narrow", axis=0, tiled=True
        )
        out_term = jnp.einsum("rc,rd->cd", context, mixed_grad, preferred_element_type=jnp.float32)
        context_grad = jnp.einsum(
            "rd,cd->rc", mixed_grad, out_full, preferred_element_type=jnp.float32
        )
        context_grad = context_grad.astype(jnp.bfloat16).reshape(
            block_count, QUERY_BLOCK, head_local, HEAD_DIM
        )
        zero_heads = jnp.zeros((row_count, head_local, HEAD_DIM), jnp.float32)
        (key_total, value_total), query_total = lax.scan(
            partial(attend_back, key_heads, value_heads, attention_scale),
            (zero_heads, zero_heads),
            (query_blocks, context_grad, same_blocks, log_total),
        )
        heads_grad = jnp.stack(
            [
                query_total.reshape(row_count, head_local * HEAD_DIM),
                key_total.reshape(row_count, head_local * HEAD_DIM),
                value_total.reshape(row_count, head_local * HEAD_DIM),
            ],
            axis=1,
        ).astype(jnp.bfloat16)
        head_bias_sum = head_bias_sum + jnp.stack(
            [
                jnp.sum(heads_grad[:, 0].astype(jnp.float32), axis=0),
                jnp.sum(heads_grad[:, 2].astype(jnp.float32), axis=0),
            ]
        )
        heads_term = jnp.einsum(
            "rd,rtc->dtc", first_normed, heads_grad, preferred_element_type=jnp.float32
        )
        first_normed_grad = lax.psum_scatter(
            heads_term_rows(heads_grad, heads_full).astype(jnp.bfloat16),
            "narrow",
            scatter_dimension=0,
            tiled=True,
        ).astype(jnp.float32)
        first_unit_part = quarter_rows(first_unit)
        first_gain_sum = first_gain_sum + jnp.sum(first_normed_grad * first_unit_part, axis=0)
        first_shift_sum = first_shift_sum + jnp.sum(first_normed_grad, axis=0)
        input_grads.append(
            (
                middle_grad
                + norm_back(
                    first_normed_grad, first_unit_part, quarter_rows(first_inverse), first_gain
                )
            ).astype(jnp.bfloat16)
        )
        term_list.append((heads_term, out_term, up_term, down_term))
    summed_terms = reduce(add_tuples, term_list)
    heads_total, out_total, up_total, down_total, head_bias_total, up_bias_total = lax.psum(
        (
            summed_terms[0],
            summed_terms[1],
            summed_terms[2],
            summed_terms[3],
            head_bias_sum,
            up_bias_sum,
        ),
        "wide",
    )
    (
        out_bias_total,
        down_bias_total,
        first_gain_total,
        first_shift_total,
        second_gain_total,
        second_shift_total,
        mixer_scale_total,
        feed_scale_total,
    ) = lax.psum(
        (
            out_bias_sum,
            down_bias_sum,
            first_gain_sum,
            first_shift_sum,
            second_gain_sum,
            second_shift_sum,
            mixer_scale_sum,
            feed_scale_sum,
        ),
        ("wide", "narrow"),
    )
    return (
        jnp.stack(outputs),
        jnp.stack(input_grads),
        heads_total,
        head_bias_total,
        out_total,
        out_bias_total,
        up_total,
        up_bias_total,
        down_total,
        down_bias_total,
        first_gain_total,
        first_shift_total,
        second_gain_total,
        second_shift_total,
        mixer_scale_total,
        feed_scale_total,
    )


def solution(mesh):
    return jax.shard_map(
        body,
        mesh=mesh,
        in_specs=(
            P(None, "wide", None),
            P(None, "wide", None),
            P("wide", None, "narrow"),
            P(None, "narrow"),
            P("narrow", "wide"),
            P(),
            P("wide", "narrow"),
            P("narrow"),
            P("narrow", "wide"),
            P(),
            P(),
            P(),
            P(),
            P(),
            P(),
            P(),
            P(None, "wide", None),
        ),
        out_specs=(
            P(None, "wide", None),
            P(None, ("wide", "narrow"), None),
            P(None, None, "narrow"),
            P(None, "narrow"),
            P("narrow", None),
            P(),
            P(None, "narrow"),
            P("narrow"),
            P("narrow", None),
            P(),
            P(),
            P(),
            P(),
            P(),
            P(),
            P(),
        ),
        check_vma=False,
    )
```

profile of v0, /device:TPU:0, one launch (start us, length us, event | category | flops | bytes accessed | tf_op | source)
XLA Modules:
  0.0 991.4 jit_solution(16991604911997666892)
XLA Ops:
  8.1 3.7 convert_reduce_fusion.2
  15.0 38.7 %all_gather.14 = bf16[768,3,192]{2,1,0:T(4,128)(2,1)S(1)} all-gather(bf16[96,3,192]{2,1,0:T(4,128)(2,1)S(1)} %copy.82), channel_id=1, replica_groups=mesh['wide'=8,'narrow'=4] {'wide'}, dimensions={0}, use_global_device_ids=true | all-gather | bytes 995328 | tf_op jit(solution)/shard_map/all_gather | solution.py:139
  54.6 3.8 fusion.231
  68.0 33.3 %all_gather.30 = bf16[192,768]{0,1:T(8,128)(2,1)} all-gather(bf16[192,96]{0,1:T(8,128)(2,1)S(1)} %copy.86), channel_id=1, replica_groups=mesh['wide'=8,'narrow'=4] {'wide'}, dimensions={1}, use_global_device_ids=true | all-gather | bytes 331776 | tf_op jit(solution)/shard_map/all_gather | solution.py:140
  120.0 23.4 %while.83 = (s32[]{:T(128)}, bf16[2,640,3,64]{1,3,2,0:T(8,128)(2,1)}, f32[2,3,640,1]{2,1,3,0:T(4,128)S(1)}, pred[2,640,1280]{2,1,0:T(8,128)(4,1)}, bf16[2,640,3,...) while((s32[]{:T(128)}, ...), condition=%wide.region_31.32_spmd, body=%wide.region_28.31_spmd.sunk | while | flops 658634880 | bytes 41280192 | solution.py:166
  121.8 3.2 fusion.390
  133.2 3.2 fusion.390
  139.4 3.2 fusion.392
  144.4 18.8 %while.82 = (s32[]{:T(128)}, bf16[2,640,3,64]{1,3,2,0:T(8,128)(2,1)}, f32[2,3,640,1]{2,1,3,0:T(4,128)S(1)}, pred[2,640,1280]{2,1,0:T(8,128)(4,1)S(1)}, bf16[2,64...) while((s32[]{:T(128)}, ...), condition=%wide.region_19.20_spmd, body=%wide.region_16.19_spmd.sunk | while | flops 658634880 | bytes 41280192 | solution.py:166
  159.2 3.2 fusion.387
  164.8 23.0 %while.81 = (s32[]{:T(128)}, bf16[2,640,3,64]{1,3,2,0:T(8,128)(2,1)}, f32[2,3,640,1]{2,1,3,0:T(4,128)S(1)}, pred[2,640,1280]{2,1,0:T(8,128)(4,1)}, bf16[2,640,3,...) while((s32[]{:T(128)}, ...), condition=%wide.region_7.8_spmd, body=%wide.region_4.7_spmd.sunk | while | flops 658634880 | bytes 41280192 | solution.py:166
  166.3 3.2 fusion.380
  172.4 3.2 fusion.382
  177.7 3.2 fusion.380
  199.3 111.8 %all-reduce.13.cloned.1.call-done = (bf16[1280,768]{1,0:T(8,128)(2,1)}, bf16[1280,768]{1,0:T(8,128)(2,1)}, bf16[1280,768]{1,0:T(8,128)(2,1)}) async-done(((bf16[1280,768]{1,0:T(8,128)(2,1)}, bf16[1280,768]{1,0:T(8,128)(2,1)}, bf16[1280,768]{1,0:T(8,128)(2,1)}), (bf16[1280,768]{1,0:T(8,128)(2,1)}, bf16[1280,768]{1,0:T(8,128)(2,1)}, bf16[1280,768]{1,0:T(8,128)(2,1)})) %all-reduce.13.cloned.1.call-update) | async-done | bytes 5898256 | tf_op jit(solution)/shard_map/psum | solution.py:171
  311.2 8.6 fusion.206
  321.8 3.9 multiply_reduce_fusion.5
  325.9 6.9 subtract_multiply_fusion.2
  332.8 13.9 %multiply_convert_fusion.5 = (bf16[1280,768]{1,0:T(8,128)(2,1)}, f32[1280,768]{1,0:T(8,128)}, f32[1280,768]{1,0:T(8,128)}) fusion(f32[768]{0:T(1024)S(1)} %copy-done.172, bf16[768,768]{1,0:T(8,128)(2,1)} %all-gather.6.cloned.1.call-done, f32[1280,768]{1,0:T(8,128)} %get-tuple-element.723, f32[768]{0:T(1024)S(1)} %copy-done.173, f32[768]{0:T(1024)S(1)} %copy-done.143), kind=kOutput, calls=%fused_computation.210 | convolution fusion | flops 1577779200 | bytes 14951424 | tf_op jit(solution)/shard_map/dot_general | solution.py:178
  346.8 7.7 convert_reduce_fusion.5
  358.9 12.5 %multiply_convert_fusion.4 = (bf16[1280,768]{1,0:T(8,128)(2,1)}, f32[1280,768]{1,0:T(8,128)S(1)}, f32[1280,768]{1,0:T(8,128)S(1)}) fusion(f32[768]{0:T(1024)S(1)} %copy-done.172, bf16[768,768]{1,0:T(8,128)(2,1)} %all-gather.6.cloned.1.call-done, f32[1280,768]{1,0:T(8,128)} %get-tuple-element.724, f32[768]{0:T(1024)S(1)} %copy-done.173, f32[768]{0:T(1024)S(1)} %copy-done.143), kind=kOutput, calls=%fused_computation.193 | convolution fusion | flops 1577779200 | bytes 14951424 | tf_op jit(solution)/shard_map/dot_general | solution.py:178
  371.4 5.2 convert_reduce_fusion.4
  381.0 12.8 %multiply_convert_fusion.3 = (bf16[1280,768]{1,0:T(8,128)(2,1)}, f32[1280,768]{1,0:T(8,128)S(1)}, f32[1280,768]{1,0:T(8,128)S(1)}) fusion(f32[768]{0:T(1024)S(1)} %copy-done.172, bf16[768,768]{1,0:T(8,128)(2,1)} %all-gather.6.cloned.1.call-done, f32[1280,768]{1,0:T(8,128)} %get-tuple-element.725, f32[768]{0:T(1024)S(1)} %copy-done.173, f32[768]{0:T(1024)S(1)} %copy-done.143), kind=kOutput, calls=%fused_computation.176 | convolution fusion | flops 1577779200 | bytes 14951424 | tf_op jit(solution)/shard_map/dot_general | solution.py:178
  393.8 5.2 convert_reduce_fusion.3
  403.4 7.5 slice_convert_fusion
  417.9 4.6 reduce-scatter.11.cloned.1.call-done
  422.6 33.4 %reduce-scatter.15.cloned.1.call-done = bf16[320,768]{1,0:T(8,128)(2,1)} async-done(((bf16[1280,768]{1,0:T(8,128)(2,1)}), bf16[320,768]{1,0:T(8,128)(2,1)}) %reduce-scatter.15.cloned.1.call-update) | async-done | bytes 491536 | tf_op jit(solution)/shard_map/reduce_scatter | solution.py:197
  456.0 3.9 fusion.196
  459.9 5.0 multiply_reduce_fusion.7
  473.4 4.8 convolution_convert_fusion.8
  484.7 4.7 convolution_convert_fusion.7
  492.5 4.6 fusion.226
  500.0 5.0 add_add_fusion
  505.0 3.4 add_add_fusion.1
  509.4 3.2 convolution_convert_fusion.9
  517.3 57.6 %while.86 = (s32[]{:T(128)}, f32[1280,3,64]{0,2,1:T(8,128)}, f32[1280,3,64]{0,2,1:T(8,128)}, bf16[2,640,3,64]{1,3,2,0:T(8,128)(2,1)}, bf16[2,640,3,64]{1,3,2,0:T...) while((s32[]{:T(128)}, f32[1280,3,64]{0,2,1:T(8,128)}, ...), condition=%wide.region_59.60_spmd.clone, body=%wide.region_57.59_spmd.clone.sunk | while | flops 1596332160 | bytes 153887056 | solution.py:229
  519.8 6.7 multiply_reduce_fusion.14
  526.6 9.8 multiply_convert_fusion.14
  536.5 5.8 fusion.430
  548.4 6.7 multiply_reduce_fusion.14
  555.1 10.0 %multiply_convert_fusion.14 = bf16[3,640,1280]{2,1,0:T(8,128)(2,1)} fusion(f32[3,640,1280]{2,1,0:T(8,128)} %get-tuple-element.1107, f32[3,640,1280]{2,1,0:T(8,128)} %copy-done, f32[3,640]{1,0:T(4,128)S(1)} %get-tuple-element.1108), kind=kLoop, calls=%fused_computation.104.clone.1 | loop fusion | flops 7372800 | bytes 24583680 | tf_op jit(solution)/shard_map/while/body/eval_jaxpr/convert_element_type | solution.py:68
  565.1 6.1 fusion.430
  574.8 3.3 convolution_convert_fusion.11
  582.8 4.5 bitcast_convert_fusion
  588.7 58.6 %while.84 = (s32[]{:T(128)}, f32[1280,3,64]{0,2,1:T(8,128)}, f32[1280,3,64]{0,2,1:T(8,128)}, bf16[2,640,3,64]{1,3,2,0:T(8,128)(2,1)}, bf16[2,640,3,64]{1,3,2,0:T...) while((s32[]{:T(128)}, f32[1280,3,64]{0,2,1:T(8,128)}, ...), condition=%wide.region_41.42_spmd.clone, body=%wide.region_39.41_spmd.clone.sunk | while | flops 1596332160 | bytes 153887056 | solution.py:229
  591.2 6.6 multiply_reduce_fusion.12
  597.8 11.1 %multiply_convert_fusion.12 = bf16[3,640,1280]{2,1,0:T(8,128)(2,1)} fusion(f32[3,640,1280]{2,1,0:T(8,128)} %get-tuple-element.1083, f32[3,640,1280]{2,1,0:T(8,128)} %copy-done.1, f32[3,640]{1,0:T(4,128)S(1)} %get-tuple-element.1084), kind=kLoop, calls=%fused_computation.48.clone.1 | loop fusion | flops 7372800 | bytes 24583680 | tf_op jit(solution)/shard_map/while/body/eval_jaxpr/convert_element_type | solution.py:68
  609.0 5.9 fusion.404
  621.0 6.6 multiply_reduce_fusion.12
  627.7 10.0 %multiply_convert_fusion.12 = bf16[3,640,1280]{2,1,0:T(8,128)(2,1)} fusion(f32[3,640,1280]{2,1,0:T(8,128)} %get-tuple-element.1083, f32[3,640,1280]{2,1,0:T(8,128)} %copy-done.1, f32[3,640]{1,0:T(4,128)S(1)} %get-tuple-element.1084), kind=kLoop, calls=%fused_computation.48.clone.1 | loop fusion | flops 7372800 | bytes 24583680 | tf_op jit(solution)/shard_map/while/body/eval_jaxpr/convert_element_type | solution.py:68
  637.6 6.0 fusion.404
  653.4 4.6 bitcast_convert_fusion.2
  659.1 58.0 %while.85 = (s32[]{:T(128)}, f32[1280,3,64]{0,2,1:T(8,128)}, f32[1280,3,64]{0,2,1:T(8,128)}, bf16[2,640,3,64]{1,3,2,0:T(8,128)(2,1)}, bf16[2,640,3,64]{1,3,2,0:T...) while((s32[]{:T(128)}, f32[1280,3,64]{0,2,1:T(8,128)}, ...), condition=%wide.region_50.51_spmd.clone, body=%wide.region_48.50_spmd.clone.sunk | while | flops 1596332160 | bytes 153887056 | solution.py:229
  661.6 6.6 multiply_reduce_fusion.13
  668.4 10.1 %multiply_convert_fusion.13 = bf16[3,640,1280]{2,1,0:T(8,128)(2,1)} fusion(f32[3,640,1280]{2,1,0:T(8,128)} %get-tuple-element.1095, f32[3,640,1280]{2,1,0:T(8,128)} %copy-done.2, f32[3,640]{1,0:T(4,128)S(1)} %get-tuple-element.1096), kind=kLoop, calls=%fused_computation.76.clone.1 | loop fusion | flops 7372800 | bytes 24583680 | tf_op jit(solution)/shard_map/while/body/eval_jaxpr/convert_element_type | solution.py:68
  678.4 5.9 fusion.417
  690.4 6.8 multiply_reduce_fusion.13
  697.6 9.8 multiply_convert_fusion.13
  707.4 6.1 fusion.417
  745.7 8.3 fusion.144
  758.3 23.9 %all-reduce.1 = (f32[2,192]{1,0:T(2,128)}, f32[768]{0:T(1024)}) all-reduce(f32[2,192]{1,0:T(2,128)S(1)} %fusion.235, f32[768]{0:T(1024)S(1)} %add_add_fusion.9), channel_id=1, replica_groups=mesh['wide'=8,'narrow'=4] {'wide'}, use_global_device_ids=true, to_apply=%region_70.71 | all-reduce | flops 1152 | bytes 9216 | tf_op jit(solution)/shard_map/psum | solution.py:270
  784.0 3.2 fusion.193
  790.4 41.3 %all-reduce = (f32[768]{0:T(1024)}, f32[768]{0:T(1024)}, f32[768]{0:T(1024)}, f32[768]{0:T(1024)}, f32[768]{0:T(1024)}, /*index=5*/f32[768]{0:T(1024)}, f32[768]{0:T(1024)}, f32[768]{0:T(1024)}) all-reduce(f32[768]{0:T(1024)S(1)} %add_multiply_fusion.1, ...), channel_id=1, replica_groups=mesh['wide'=8,'narrow'=4] {'wide','narrow'}, use_global_device_ids=true, to_apply=%region_75.76 | all-reduce | flops 6144 | bytes 49152 | tf_op jit(solution)/shard_map/psum | solution.py:290
  835.5 141.7 %all-reduce.9.cloned.1.call-done = (f32[768,3,192]{0,2,1:T(8,128)}, f32[192,768]{1,0:T(8,128)}, f32[768,768]{1,0:T(8,128)}, f32[768,768]{1,0:T(8,128)}) async-done(((f32[768,3,192]{0,2,1:T(8,128)}, f32[192,768]{1,0:T(8,128)}, f32[768,768]{1,0:T(8,128)}, f32[768,768]{1,0:T(8,128)}), (f32[768,3,192]{0,2,1:T(8,128)}, f32[192,768]{1,0:T(8,128)}, f32[768,768]{1,0:T(8,128)}, ...) | async-done | bytes 7077904 | tf_op jit(solution)/shard_map/psum | solution.py:270
  (695 shorter events, 233.7 us)
Async XLA Ops:
  8.0 303.1 %all-reduce.13.cloned.1.call-start = ((), (), s32[]{:S(2)}) async-start(), calls=%async_computation.19 | async-start | bytes 11796480 | tf_op jit(solution)/shard_map/psum | solution.py:171
  11.8 51.1 %copy-start.122 = (f32[1280]{0:T(1024)}, f32[1280]{0:T(1024)S(1)}, u32[]{:S(2)}) copy-start(f32[1280]{0:T(1024)S(1)} %broadcast_multiply_fusion.5) | copy-start | bytes 15364
  11.8 42.7 %copy-start.125 = (f32[1280]{0:T(1024)}, f32[1280]{0:T(1024)S(1)}, u32[]{:S(2)}) copy-start(f32[1280]{0:T(1024)S(1)} %get-tuple-element.769) | copy-start | bytes 15364
  11.9 48.0 %copy-start.128 = (f32[1280]{0:T(1024)}, f32[1280]{0:T(1024)S(1)}, u32[]{:S(2)}) copy-start(f32[1280]{0:T(1024)S(1)} %get-tuple-element.770) | copy-start | bytes 15364
  12.5 42.1 %copy-start.131 = (f32[768]{0:T(1024)S(1)}, f32[768]{0:T(1024)}, u32[]{:S(2)}) copy-start(f32[768]{0:T(1024)} %param.39) | copy-start | bytes 9220
  12.5 42.1 %copy-start.174 = (f32[768]{0:T(1024)S(1)}, f32[768]{0:T(1024)}, u32[]{:S(2)}) copy-start(f32[768]{0:T(1024)} %param.40) | copy-start | bytes 9220
  14.8 43.5 %copy-start.134 = (f32[1280]{0:T(1024)}, f32[1280]{0:T(1024)S(1)}, u32[]{:S(2)}) copy-start(f32[1280]{0:T(1024)S(1)} %add_rsqrt_fusion.1) | copy-start | bytes 15364
  54.5 8.4 copy-start.108
  144.4 19.7 %copy-start.9 = (bf16[1280,1,192]{0,2,1:T(8,128)(2,1)S(1)}, bf16[1280,1,192]{0,2,1:T(8,128)(2,1)}, u32[]{:S(2)}) copy-start(bf16[1280,1,192]{0,2,1:T(8,128)(2,1)} %slice.187) | copy-start | bytes 1474564
  196.0 115.2 %copy-start.117 = (f32[768]{0:T(1024)S(1)}, f32[768]{0:T(1024)}, u32[]{:S(2)}) copy-start(f32[768]{0:T(1024)} %param.43) | copy-start | bytes 9220
  196.0 115.2 %copy-start.120 = (f32[768]{0:T(1024)S(1)}, f32[768]{0:T(1024)}, u32[]{:S(2)}) copy-start(f32[768]{0:T(1024)} %param.34) | copy-start | bytes 9220
  196.0 115.1 %copy-start.126 = (f32[1280]{0:T(1024)S(1)}, f32[1280]{0:T(1024)}, u32[]{:S(2)}) copy-start(f32[1280]{0:T(1024)} %copy-done.125) | copy-start | bytes 15364
  196.0 115.1 %copy-start.129 = (f32[1280]{0:T(1024)S(1)}, f32[1280]{0:T(1024)}, u32[]{:S(2)}) copy-start(f32[1280]{0:T(1024)} %copy-done.128) | copy-start | bytes 15364
  196.0 115.1 %copy-start.135 = (f32[1280]{0:T(1024)S(1)}, f32[1280]{0:T(1024)}, u32[]{:S(2)}) copy-start(f32[1280]{0:T(1024)} %copy-done.134) | copy-start | bytes 15364
  196.0 115.1 %copy-start.138 = (f32[1280]{0:T(1024)S(1)}, f32[1280]{0:T(1024)}, u32[]{:S(2)}) copy-start(f32[1280]{0:T(1024)} %copy-done.137) | copy-start | bytes 15364
  198.0 134.7 %all-gather.6.cloned.1.call-start = ((), (), s32[]{:S(2)}) async-start(), calls=%async_computation.6 | async-start | bytes 1327104 | tf_op jit(solution)/shard_map/all_gather | solution.py:141
  198.6 148.1 %all-gather.8.cloned.1.call-start = ((), (), s32[]{:S(2)}) async-start(), calls=%async_computation.7 | async-start | bytes 1327104 | tf_op jit(solution)/shard_map/all_gather | solution.py:142
  199.2 218.7 %reduce-scatter.7.cloned.1.call-start = ((), (), s32[]{:S(2)}) async-start(), calls=%async_computation.8 | async-start | bytes 2457600 | tf_op jit(solution)/shard_map/reduce_scatter | solution.py:197
  311.1 8.7 slice-start.2
  311.1 8.7 slice-start.3
  311.2 9.4 copy-start.17
  311.2 10.1 %copy-start.19 = (bf16[1280,768]{1,0:T(8,128)(2,1)S(1)}, bf16[1280,768]{1,0:T(8,128)(2,1)}, u32[]{:S(2)}) copy-start(bf16[1280,768]{1,0:T(8,128)(2,1)} %get-tuple-element.697) | copy-start | bytes 5898244
  311.2 10.7 %copy-start.21 = (bf16[1280,768]{1,0:T(8,128)(2,1)S(1)}, bf16[1280,768]{1,0:T(8,128)(2,1)}, u32[]{:S(2)}) copy-start(bf16[1280,768]{1,0:T(8,128)(2,1)} %get-tuple-element.698) | copy-start | bytes 5898244
  325.8 6.9 copy-start.143
  325.8 6.9 copy-start.172
  325.9 6.9 copy-start.173
  332.8 14.0 %copy-start.145 = (f32[768]{0:T(1024)S(1)}, f32[768]{0:T(1024)}, u32[]{:S(2)}) copy-start(f32[768]{0:T(1024)} %param.44) | copy-start | bytes 9220
  346.8 9.0 copy-start.169
  358.9 63.7 %reduce-scatter.11.cloned.1.call-start = ((), (), s32[]{:S(2)}) async-start(), calls=%async_computation.11 | async-start | bytes 2457600 | tf_op jit(solution)/shard_map/reduce_scatter | solution.py:197
  358.9 12.5 %copy-start.168 = (bf16[768,768]{0,1:T(8,128)(2,1)S(1)}, bf16[768,768]{0,1:T(8,128)(2,1)}, u32[]{:S(2)}) copy-start(bf16[768,768]{0,1:T(8,128)(2,1)} %all-gather.8.cloned.1.call-done) | copy-start | bytes 3538948
  380.9 75.0 %reduce-scatter.15.cloned.1.call-start = ((), (), s32[]{:S(2)}) async-start(), calls=%async_computation.14 | async-start | bytes 2457600 | tf_op jit(solution)/shard_map/reduce_scatter | solution.py:197
  403.3 105.4 %all-gather.14.cloned.1.call-start = ((), (), s32[]{:S(2)}) async-start(), calls=%async_computation.15 | async-start | bytes 2457600 | tf_op jit(solution)/shard_map/all_gather | solution.py:218
  417.9 42.0 %copy-start.87 = (bf16[320,768]{1,0:T(8,128)(2,1)S(1)}, bf16[320,768]{1,0:T(8,128)(2,1)}, u32[]{:S(2)}) copy-start(bf16[320,768]{1,0:T(8,128)(2,1)} %reduce-scatter.7.cloned.1.call-done) | copy-start | bytes 1474564
  422.6 37.3 %copy-start.88 = (bf16[320,768]{1,0:T(8,128)(2,1)S(1)}, bf16[320,768]{1,0:T(8,128)(2,1)}, u32[]{:S(2)}) copy-start(bf16[320,768]{1,0:T(8,128)(2,1)} %reduce-scatter.11.cloned.1.call-done) | copy-start | bytes 1474564
  465.9 12.3 %slice-start.6 = ((s8[5898240]{0:T(1024)(128)(4,1)}), s8[1703936]{0:T(1024)(128)(4,1)S(1)}, s32[]{:S(2)}) async-start(s8[5898240]{0:T(1024)(128)(4,1)} %bitcast.559), calls=%async_computation.26 | async-start | bytes 3407872
  467.1 107.7 %all-gather.10.cloned.1.call-start = ((), (), s32[]{:S(2)}) async-start(), calls=%async_computation.9 | async-start | bytes 2457600 | tf_op jit(solution)/shard_map/all_gather | solution.py:218
  467.7 179.6 %all-gather.12.cloned.1.call-start = ((), (), s32[]{:S(2)}) async-start(), calls=%async_computation.12 | async-start | bytes 2457600 | tf_op jit(solution)/shard_map/all_gather | solution.py:218
  484.7 240.1 %all-reduce.11.cloned.1.call-start = ((), (), s32[]{:S(2)}) async-start(), calls=%async_computation.18 | async-start | bytes 11796480 | tf_op jit(solution)/shard_map/psum | solution.py:181
  508.4 8.9 copy-start.12
  508.4 8.8 copy-start.16
  508.4 8.8 copy-start.26
  508.4 8.8 copy-start.43
  508.4 8.8 copy-start.112
  508.4 273.7 %reduce-scatter.17.cloned.1.call-start = ((), (), s32[]{:S(2)}) async-start(), calls=%async_computation.16 | async-start | bytes 2457600 | tf_op jit(solution)/shard_map/reduce_scatter | solution.py:251
  519.8 6.8 copy-start
  548.4 6.7 copy-start
  574.8 6.9 copy-start.28
  574.8 7.0 copy-start.37
  587.4 196.5 %reduce-scatter.9.cloned.1.call-start = ((), (), s32[]{:S(2)}) async-start(), calls=%async_computation.10 | async-start | bytes 2457600 | tf_op jit(solution)/shard_map/reduce_scatter | solution.py:251
  621.0 6.7 copy-start.1
  658.0 129.3 %reduce-scatter.13.cloned.1.call-start = ((), (), s32[]{:S(2)}) async-start(), calls=%async_computation.13 | async-start | bytes 2457600 | tf_op jit(solution)/shard_map/reduce_scatter | solution.py:251
  661.6 6.8 copy-start.2
  690.4 7.2 copy-start.2
  719.1 12.8 %copy-start.74 = (bf16[1280,1,192]{0,2,1:T(8,128)(2,1)}, bf16[1280,1,192]{0,2,1:T(8,128)(2,1)S(1)}, u32[]{:S(2)}) copy-start(bf16[1280,1,192]{0,2,1:T(8,128)(2,1)S(1)} %stack_reshape.39) | copy-start | bytes 1474564
  720.5 11.4 %copy-start.72 = (bf16[1280,3,64]{0,2,1:T(8,128)(2,1)}, bf16[1280,3,64]{0,2,1:T(8,128)(2,1)S(1)}, u32[]{:S(2)}) copy-start(bf16[1280,3,64]{0,2,1:T(8,128)(2,1)S(1)} %convert.53) | copy-start | bytes 1474564
  724.5 252.7 %all-reduce.9.cloned.1.call-start = ((), (), s32[]{:S(2)}) async-start(), calls=%async_computation.17 | async-start | bytes 14155776 | tf_op jit(solution)/shard_map/psum | solution.py:270
  757.2 26.8 %copy-start.51 = (f32[320,768]{1,0:T(8,128)S(1)}, f32[320,768]{1,0:T(8,128)}, u32[]{:S(2)}) copy-start(f32[320,768]{1,0:T(8,128)} %copy-done.50) | copy-start | bytes 2949124
  757.2 26.8 %copy-start.161 = (f32[320]{0:T(512)S(1)}, f32[320]{0:T(512)}, u32[]{:S(2)}) copy-start(f32[320]{0:T(512)} %dynamic-slice.26) | copy-start | bytes 3844
  757.6 29.6 %copy-start.49 = (f32[320,768]{1,0:T(8,128)S(1)}, f32[320,768]{1,0:T(8,128)}, u32[]{:S(2)}) copy-start(f32[320,768]{1,0:T(8,128)} %copy-done.48) | copy-start | bytes 2949124
  757.6 29.6 %copy-start.160 = (f32[320]{0:T(512)S(1)}, f32[320]{0:T(512)}, u32[]{:S(2)}) copy-start(f32[320]{0:T(512)} %dynamic-slice.22) | copy-start | bytes 3844
  784.0 47.7 %copy-start.53 = (f32[320,768]{1,0:T(8,128)S(1)}, f32[320,768]{1,0:T(8,128)}, u32[]{:S(2)}) copy-start(f32[320,768]{1,0:T(8,128)} %copy-done.52) | copy-start | bytes 2949124
  784.0 47.7 %copy-start.162 = (f32[320]{0:T(512)S(1)}, f32[320]{0:T(512)}, u32[]{:S(2)}) copy-start(f32[320]{0:T(512)} %dynamic-slice.24) | copy-start | bytes 3844
  787.2 46.0 %copy-start.90 = (bf16[1,320,768]{2,1,0:T(8,128)(2,1)S(1)}, bf16[1,320,768]{2,1,0:T(8,128)(2,1)}, u32[]{:S(2)}) copy-start(bf16[1,320,768]{2,1,0:T(8,128)(2,1)} %get-tuple-element.739) | copy-start | bytes 1474564
  787.3 44.5 %copy-start.84 = (bf16[320,768]{1,0:T(8,128)(2,1)S(1)}, bf16[320,768]{1,0:T(8,128)(2,1)}, u32[]{:S(2)}) copy-start(bf16[320,768]{1,0:T(8,128)(2,1)} %reduce-scatter.13.cloned.1.call-done) | copy-start | bytes 1474564
  (171 other events, 538.6 us)
Sparse Core Ops, SparseCore 0:
  198.2 112.8 all-reduce.12
  359.0 30.5 reduce-scatter.6
  392.1 30.3 reduce-scatter.10
  425.5 30.3 reduce-scatter.14
  467.2 21.8 all-gather.13
  491.1 21.8 all-gather.9
  514.5 21.8 all-gather.11
  539.0 113.2 all-reduce.10
  654.8 30.5 reduce-scatter.16
  687.8 30.3 reduce-scatter.8
  724.6 30.2 reduce-scatter.12
Sparse Core Ops, SparseCore 1:
  200.7 40.8 all-gather.5
  243.6 39.8 all-gather.7
  744.3 232.9 all-reduce.8
where the time goes:
time: 999 us; the launch traced here: 991 us
  waiting for transfers between devices  293 us (29%)
  matrix products  284 us (28%)
  other arithmetic  175 us (18%)
  blocking collectives  137 us (14%)
  local copies, waits for them, and re-layouts  79.8 us (8%)
  between operations  17.9 us (2%)
    psum x1, waiting for transfers between devices, body(): lax.psum((summed_terms[0], summed_terms[1], summed_terms[2], summed_terms...  142 us
    psum x1, waiting for transfers between devices, body(): lax.psum(jnp.dot(context, out_full, preferred_element_type=jnp.float32).a...  112 us
    convert_element_type x6, other arithmetic, attend_back(): score_grad = (soft_weights * (weight_grad - row_delta)).astype(jnp.bfloat16)  60.8 us
    psum x1, blocking collectives, body(): lax.psum((out_bias_sum, down_bias_sum, first_gain_sum, first_shift_sum, s...  41.3 us
    dot_general x6, matrix products, attend_back(): jnp.einsum('qhc,khc->hqk', query_heads, key_heads, preferred_element_type...  40 us
    dot_general x3, matrix products, body(): jnp.dot(second_normed, up_full, preferred_element_type=jnp.float32)  39.2 us
    all_gather x1, blocking collectives, body(): lax.all_gather(heads_weight, 'wide', axis=0, tiled=True)  38.7 us
    reduce_scatter x3, waiting for transfers between devices, body(): lax.psum_scatter(feed_term(upper_grad, up_full).astype(jnp.bfloat16), 'na...  38 us
  transfers between devices with their start and end apart: 14, of which 4 were waited for; matrix products, arithmetic and copies ran while one was open for 38% of the time, Pallas kernels for 0%

commit v1 on v0

--- a/solution.py
+++ b/solution.py
@@ -168,9 +168,12 @@
             (query_blocks, same_blocks),
         )
         context = context_blocks.reshape(row_count, head_local * HEAD_DIM).astype(jnp.bfloat16)
-        mixed = lax.psum(
-            jnp.dot(context, out_full, preferred_element_type=jnp.float32).astype(jnp.bfloat16),
-            "narrow",
+        mixed = jnp.sum(
+            lax.all_gather(
+                jnp.dot(context, out_full, preferred_element_type=jnp.float32).astype(jnp.bfloat16),
+                "narrow",
+            ),
+            axis=0,
         ).astype(jnp.float32)
         middle = token_rows + mixer_scale * (mixed + out_bias)
         second_unit, second_inverse = norm_parts(middle)

time: 999 us -> 1070 us (1.071)
  waiting for transfers between devices: 293 us -> 346 us
  other arithmetic: 175 us -> 194 us
    psum x1 -> x0, waiting for transfers between devices: 112 us -> none  [body(): lax.psum(jnp.dot(context, out_full, preferred_element_type=jnp.float32).a...]
    all_gather x0 -> x3, waiting for transfers between devices: none -> 105 us  [body(): lax.all_gather(jnp.dot(context, out_full, preferred_element_type=jnp.floa...]
    all_gather x1, waiting for transfers between devices: 0.03 us -> 27.7 us  [body(): lax.all_gather(down_weight, 'wide', axis=1, tiled=True)]
    reduce_sum x0 -> x3, other arithmetic: none -> 18.8 us  [body(): jnp.sum(lax.all_gather(jnp.dot(context, out_full, preferred_element_type=...]
    psum x1, waiting for transfers between devices: 142 us -> 158 us  [body(): lax.psum((summed_terms[0], summed_terms[1], summed_terms[2], summed_terms...]
    all_gather x1, waiting for transfers between devices: 0.01 us -> 15.4 us  [body(): lax.all_gather(up_weight, 'wide', axis=0, tiled=True)]
    unnamed x346 -> x356, local copies, waits for them, and re-layouts: 29.4 us -> 34 us
  transfers between devices with their start and end apart: 14 -> 16, of which waited for: 4 -> 8; matrix products, arithmetic and copies ran while one was open for 38% -> 41% of each run, Pallas kernels for 0% -> 0%
where the time goes in v1:
time: 1070 us; the launch traced here: 1060 us
  waiting for transfers between devices  346 us (32%)
  matrix products  284 us (27%)
  other arithmetic  194 us (18%)
  blocking collectives  136 us (13%)
  local copies, waits for them, and re-layouts  80.8 us (8%)
  between operations  16.4 us (2%)
    psum x1, waiting for transfers between devices, body(): lax.psum((summed_terms[0], summed_terms[1], summed_terms[2], summed_terms...  158 us
    all_gather x3, waiting for transfers between devices, body(): lax.all_gather(jnp.dot(context, out_full, preferred_element_type=jnp.floa...  105 us
    convert_element_type x6, other arithmetic, attend_back(): score_grad = (soft_weights * (weight_grad - row_delta)).astype(jnp.bfloat16)  61.2 us
    psum x1, blocking collectives, body(): lax.psum((out_bias_sum, down_bias_sum, first_gain_sum, first_shift_sum, s...  42.3 us
    dot_general x6, matrix products, attend_back(): jnp.einsum('qhc,khc->hqk', query_heads, key_heads, preferred_element_type...  39.8 us
    all_gather x1, blocking collectives, body(): lax.all_gather(heads_weight, 'wide', axis=0, tiled=True)  38.7 us
    dot_general x3, matrix products, body(): jnp.dot(second_normed, up_full, preferred_element_type=jnp.float32)  38.5 us
    reduce_scatter x3, waiting for transfers between devices, body(): lax.psum_scatter(feed_term(upper_grad, up_full).astype(jnp.bfloat16), 'na...  37.6 us
  transfers between devices with their start and end apart: 16, of which 8 were waited for; matrix products, arithmetic and copies ran while one was open for 41% of the time, Pallas kernels for 0%

profile of v1, /device:TPU:0, one launch (start us, length us, event | category | flops | bytes accessed | tf_op | source)
XLA Modules:
  0.0 1060.0 jit_solution(14814149824895746084)
XLA Ops:
  7.2 3.7 convert_reduce_fusion.2
  14.2 38.7 %all_gather.47 = bf16[768,3,192]{2,1,0:T(4,128)(2,1)S(1)} all-gather(bf16[96,3,192]{2,1,0:T(4,128)(2,1)S(1)} %copy.82), channel_id=1, replica_groups=mesh['wide'=8,'narrow'=4] {'wide'}, dimensions={0}, use_global_device_ids=true | all-gather | bytes 995328 | tf_op jit(solution)/shard_map/all_gather | solution.py:139
  53.7 3.7 fusion.231
  60.9 31.2 %all_gather.48 = bf16[192,768]{0,1:T(8,128)(2,1)S(1)} all-gather(bf16[192,96]{0,1:T(8,128)(2,1)S(1)} %copy.86), channel_id=1, replica_groups=mesh['wide'=8,'narrow'=4] {'wide'}, dimensions={1}, use_global_device_ids=true | all-gather | bytes 331776 | tf_op jit(solution)/shard_map/all_gather | solution.py:140
  96.5 3.9 fusion.228
  106.0 3.7 fusion.225
  121.8 18.8 %while.83 = (s32[]{:T(128)}, bf16[2,640,3,64]{1,3,2,0:T(8,128)(2,1)}, f32[2,3,640,1]{2,1,3,0:T(4,128)S(1)}, pred[2,640,1280]{2,1,0:T(8,128)(4,1)S(1)}, bf16[2,64...) while((s32[]{:T(128)}, ...), condition=%wide.region_31.32_spmd, body=%wide.region_28.31_spmd.sunk | while | flops 658634880 | bytes 41280192 | solution.py:166
  149.0 18.6 %while.82 = (s32[]{:T(128)}, bf16[2,640,3,64]{1,3,2,0:T(8,128)(2,1)}, f32[2,3,640,1]{2,1,3,0:T(4,128)S(1)}, pred[2,640,1280]{2,1,0:T(8,128)(4,1)S(1)}, bf16[2,64...) while((s32[]{:T(128)}, ...), condition=%wide.region_19.20_spmd, body=%wide.region_16.19_spmd.sunk | while | flops 658634880 | bytes 41280192 | solution.py:166
  176.1 17.1 %while.81 = (s32[]{:T(128)}, bf16[2,640,3,64]{1,3,2,0:T(8,128)(2,1)S(1)}, f32[2,3,640,1]{2,1,3,0:T(4,128)S(1)}, pred[2,640,1280]{2,1,0:T(8,128)(4,1)S(1)}, bf16[...) while((s32[]{:T(128)}, ...), condition=%wide.region_7.8_spmd, body=%wide.region_4.7_spmd.sunk | while | flops 658634880 | bytes 37347976 | solution.py:166
  200.3 6.2 reduce_sum.645
  206.5 51.2 %all-gather.24.cloned.1.call-done = bf16[5120,768]{1,0:T(8,128)(2,1)} async-done(((bf16[1280,768]{1,0:T(8,128)(2,1)}), bf16[5120,768]{1,0:T(8,128)(2,1)}) %all-gather.24.cloned.1.call-update) | async-done | bytes 7864336 | tf_op jit(solution)/shard_map/all_gather | solution.py:172
  257.7 6.2 reduce_sum.639
  263.9 51.3 %all-gather.22.cloned.1.call-done = bf16[5120,768]{1,0:T(8,128)(2,1)} async-done(((bf16[1280,768]{1,0:T(8,128)(2,1)}), bf16[5120,768]{1,0:T(8,128)(2,1)}) %all-gather.22.cloned.1.call-update) | async-done | bytes 7864336 | tf_op jit(solution)/shard_map/all_gather | solution.py:172
  315.2 6.4 reduce_sum.633
  321.7 8.6 fusion.206
  332.1 3.9 multiply_reduce_fusion.5
  336.1 6.8 subtract_multiply_fusion.2
  343.0 15.4 %all-gather.12.cloned.1.call-done = bf16[768,768]{1,0:T(8,128)(2,1)} async-done(((bf16[96,768]{1,0:T(8,128)(2,1)}), bf16[768,768]{1,0:T(8,128)(2,1)}) %all-gather.12.cloned.1.call-update) | async-done | bytes 1179664 | tf_op jit(solution)/shard_map/all_gather | solution.py:141
  358.4 14.2 %multiply_convert_fusion.5 = (bf16[1280,768]{1,0:T(8,128)(2,1)}, f32[1280,768]{1,0:T(8,128)}, f32[1280,768]{1,0:T(8,128)}) fusion(f32[768]{0:T(1024)S(1)} %copy-done.175, bf16[768,768]{1,0:T(8,128)(2,1)} %all-gather.12.cloned.1.call-done, f32[1280,768]{1,0:T(8,128)} %get-tuple-element.720, f32[768]{0:T(1024)S(1)} %copy-done.176, f32[768]{0:T(1024)S(1)} %copy-done.145), kind=kOutput, calls=%fused_computation.210 | convolution fusion | flops 1577779200 | bytes 14951424 | tf_op jit(solution)/shard_map/dot_general | solution.py:181
  372.6 27.7 %all-gather.14.cloned.1.call-done = bf16[768,768]{0,1:T(8,128)(2,1)} async-done(((bf16[768,96]{0,1:T(8,128)(2,1)}), bf16[768,768]{0,1:T(8,128)(2,1)}) %all-gather.14.cloned.1.call-update) | async-done | bytes 1179664 | tf_op jit(solution)/shard_map/all_gather | solution.py:142
  400.2 7.7 convert_reduce_fusion.5
  412.4 12.1 %multiply_convert_fusion.4 = (bf16[1280,768]{1,0:T(8,128)(2,1)}, f32[1280,768]{1,0:T(8,128)S(1)}, f32[1280,768]{1,0:T(8,128)S(1)}) fusion(f32[768]{0:T(1024)S(1)} %copy-done.175, bf16[768,768]{1,0:T(8,128)(2,1)S(1)} %copy-done.174, f32[1280,768]{1,0:T(8,128)} %get-tuple-element.721, f32[768]{0:T(1024)S(1)} %copy-done.176, f32[768]{0:T(1024)S(1)} %copy-done.145), kind=kOutput, calls=%fused_computation.193 | convolution fusion | flops 1577779200 | bytes 14951424 | tf_op jit(solution)/shard_map/dot_general | solution.py:181
  424.5 5.1 convert_reduce_fusion.4
  433.9 12.2 %multiply_convert_fusion.3 = (bf16[1280,768]{1,0:T(8,128)(2,1)}, f32[1280,768]{1,0:T(8,128)S(1)}, f32[1280,768]{1,0:T(8,128)S(1)}) fusion(f32[768]{0:T(1024)S(1)} %copy-done.175, bf16[768,768]{1,0:T(8,128)(2,1)S(1)} %copy-done.174, f32[1280,768]{1,0:T(8,128)} %get-tuple-element.722, f32[768]{0:T(1024)S(1)} %copy-done.176, f32[768]{0:T(1024)S(1)} %copy-done.145), kind=kOutput, calls=%fused_computation.176 | convolution fusion | flops 1577779200 | bytes 14951424 | tf_op jit(solution)/shard_map/dot_general | solution.py:181
  446.2 5.1 convert_reduce_fusion.3
  455.6 7.6 slice_convert_fusion
  470.4 4.1 reduce-scatter.11.cloned.1.call-done
  474.5 33.5 %reduce-scatter.15.cloned.1.call-done = bf16[320,768]{1,0:T(8,128)(2,1)} async-done(((bf16[1280,768]{1,0:T(8,128)(2,1)}), bf16[320,768]{1,0:T(8,128)(2,1)}) %reduce-scatter.15.cloned.1.call-update) | async-done | bytes 491536 | tf_op jit(solution)/shard_map/reduce_scatter | solution.py:200
  508.0 3.9 fusion.196
  512.0 5.0 multiply_reduce_fusion.7
  525.7 4.8 convolution_convert_fusion.8
  537.0 4.7 convolution_convert_fusion.7
  544.8 4.6 fusion.226
  552.7 5.0 add_add_fusion
  557.8 3.4 add_add_fusion.1
  570.1 57.4 %while.86 = (s32[]{:T(128)}, f32[1280,3,64]{0,2,1:T(8,128)}, f32[1280,3,64]{0,2,1:T(8,128)}, bf16[2,640,3,64]{1,3,2,0:T(8,128)(2,1)}, bf16[2,640,3,64]{1,3,2,0:T...) while((s32[]{:T(128)}, f32[1280,3,64]{0,2,1:T(8,128)}, ...), condition=%wide.region_59.60_spmd.clone, body=%wide.region_57.59_spmd.clone.sunk | while | flops 1596332160 | bytes 153887056 | solution.py:232
  572.6 6.7 multiply_reduce_fusion.14
  579.3 9.8 multiply_convert_fusion.14
  589.2 5.8 fusion.430
  601.1 6.8 multiply_reduce_fusion.14
  607.9 9.9 multiply_convert_fusion.14
  617.8 6.1 fusion.430
  627.5 3.4 convolution_convert_fusion.11
  635.6 4.5 bitcast_convert_fusion
  641.2 58.7 %while.84 = (s32[]{:T(128)}, f32[1280,3,64]{0,2,1:T(8,128)}, f32[1280,3,64]{0,2,1:T(8,128)}, bf16[2,640,3,64]{1,3,2,0:T(8,128)(2,1)}, bf16[2,640,3,64]{1,3,2,0:T...) while((s32[]{:T(128)}, f32[1280,3,64]{0,2,1:T(8,128)}, ...), condition=%wide.region_41.42_spmd.clone, body=%wide.region_39.41_spmd.clone.sunk | while | flops 1596332160 | bytes 153887056 | solution.py:232
  643.8 6.6 multiply_reduce_fusion.12
  650.4 11.3 %multiply_convert_fusion.12 = bf16[3,640,1280]{2,1,0:T(8,128)(2,1)} fusion(f32[3,640,1280]{2,1,0:T(8,128)} %get-tuple-element.1080, f32[3,640,1280]{2,1,0:T(8,128)} %copy-done.1, f32[3,640]{1,0:T(4,128)S(1)} %get-tuple-element.1081), kind=kLoop, calls=%fused_computation.48.clone.1 | loop fusion | flops 7372800 | bytes 24583680 | tf_op jit(solution)/shard_map/while/body/eval_jaxpr/convert_element_type | solution.py:68
  661.7 5.9 fusion.404
  673.7 6.6 multiply_reduce_fusion.12
  680.3 10.0 multiply_convert_fusion.12
  690.3 6.0 fusion.404
  706.0 4.5 bitcast_convert_fusion.2
  711.9 58.3 %while.85 = (s32[]{:T(128)}, f32[1280,3,64]{0,2,1:T(8,128)}, f32[1280,3,64]{0,2,1:T(8,128)}, bf16[2,640,3,64]{1,3,2,0:T(8,128)(2,1)}, bf16[2,640,3,64]{1,3,2,0:T...) while((s32[]{:T(128)}, f32[1280,3,64]{0,2,1:T(8,128)}, ...), condition=%wide.region_50.51_spmd.clone, body=%wide.region_48.50_spmd.clone.sunk | while | flops 1596332160 | bytes 153887056 | solution.py:232
  714.4 6.6 multiply_reduce_fusion.13
  721.0 10.1 multiply_convert_fusion.13
  731.1 5.9 fusion.417
  743.1 6.6 multiply_reduce_fusion.13
  750.3 10.1 multiply_convert_fusion.13
  760.4 6.1 fusion.417
  798.9 7.5 fusion.144
  810.6 23.6 %all-reduce.1 = (f32[2,192]{1,0:T(2,128)}, f32[768]{0:T(1024)}) all-reduce(f32[2,192]{1,0:T(2,128)S(1)} %fusion.235, f32[768]{0:T(1024)S(1)} %add_add_fusion.9), channel_id=1, replica_groups=mesh['wide'=8,'narrow'=4] {'wide'}, use_global_device_ids=true, to_apply=%region_70.71 | all-reduce | flops 1152 | bytes 9216 | tf_op jit(solution)/shard_map/psum | solution.py:273
  836.0 3.3 fusion.193
  842.6 42.3 %all-reduce = (f32[768]{0:T(1024)}, f32[768]{0:T(1024)}, f32[768]{0:T(1024)}, f32[768]{0:T(1024)}, f32[768]{0:T(1024)}, /*index=5*/f32[768]{0:T(1024)}, f32[768]{0:T(1024)}, f32[768]{0:T(1024)}) all-reduce(f32[768]{0:T(1024)S(1)} %add_multiply_fusion.1, ...), channel_id=1, replica_groups=mesh['wide'=8,'narrow'=4] {'wide','narrow'}, use_global_device_ids=true, to_apply=%region_75.76 | all-reduce | flops 6144 | bytes 49152 | tf_op jit(solution)/shard_map/psum | solution.py:293
  888.7 158.0 %all-reduce.7.cloned.1.call-done = (f32[768,3,192]{0,2,1:T(8,128)}, f32[192,768]{1,0:T(8,128)}, f32[768,768]{1,0:T(8,128)}, f32[768,768]{1,0:T(8,128)}) async-done(((f32[768,3,192]{0,2,1:T(8,128)}, f32[192,768]{1,0:T(8,128)}, f32[768,768]{1,0:T(8,128)}, f32[768,768]{1,0:T(8,128)}), (f32[768,3,192]{0,2,1:T(8,128)}, f32[192,768]{1,0:T(8,128)}, f32[768,768]{1,0:T(8,128)}, ...) | async-done | bytes 7077904 | tf_op jit(solution)/shard_map/psum | solution.py:273
  (705 shorter events, 257.1 us)
Async XLA Ops:
  7.2 193.1 %all-gather.26.cloned.1.call-start = ((), (), s32[]{:S(2)}) async-start(), calls=%async_computation.19 | async-start | bytes 9830400 | tf_op jit(solution)/shard_map/all_gather | solution.py:172
  11.0 95.0 %copy-start.124 = (f32[1280]{0:T(1024)}, f32[1280]{0:T(1024)S(1)}, u32[]{:S(2)}) copy-start(f32[1280]{0:T(1024)S(1)} %broadcast_multiply_fusion.5) | copy-start | bytes 15364
  11.0 42.7 %copy-start.127 = (f32[1280]{0:T(1024)}, f32[1280]{0:T(1024)S(1)}, u32[]{:S(2)}) copy-start(f32[1280]{0:T(1024)S(1)} %get-tuple-element.766) | copy-start | bytes 15364
  11.0 85.4 %copy-start.130 = (f32[1280]{0:T(1024)}, f32[1280]{0:T(1024)S(1)}, u32[]{:S(2)}) copy-start(f32[1280]{0:T(1024)S(1)} %get-tuple-element.767) | copy-start | bytes 15364
  11.7 42.1 %copy-start.133 = (f32[768]{0:T(1024)S(1)}, f32[768]{0:T(1024)}, u32[]{:S(2)}) copy-start(f32[768]{0:T(1024)} %param.39) | copy-start | bytes 9220
  11.7 42.1 %copy-start.177 = (f32[768]{0:T(1024)S(1)}, f32[768]{0:T(1024)}, u32[]{:S(2)}) copy-start(f32[768]{0:T(1024)} %param.40) | copy-start | bytes 9220
  14.0 43.4 %copy-start.136 = (f32[1280]{0:T(1024)}, f32[1280]{0:T(1024)S(1)}, u32[]{:S(2)}) copy-start(f32[1280]{0:T(1024)S(1)} %add_rsqrt_fusion.1) | copy-start | bytes 15364
  60.8 45.2 %copy-start.142 = (f32[1280]{0:T(1024)}, f32[1280]{0:T(1024)S(1)}, u32[]{:S(2)}) copy-start(f32[1280]{0:T(1024)S(1)} %add_rsqrt_fusion.5) | copy-start | bytes 15364
  60.8 39.5 %copy-start.139 = (f32[1280]{0:T(1024)}, f32[1280]{0:T(1024)S(1)}, u32[]{:S(2)}) copy-start(f32[1280]{0:T(1024)S(1)} %add_rsqrt_fusion.3) | copy-start | bytes 15364
  92.1 101.8 %copy-start.49 = (bf16[192,768]{0,1:T(8,128)(2,1)}, bf16[192,768]{0,1:T(8,128)(2,1)S(1)}, u32[]{:S(2)}) copy-start(bf16[192,768]{0,1:T(8,128)(2,1)S(1)} %all_gather.48) | copy-start | bytes 884740
  140.6 7.5 copy-start.30
  140.6 8.3 copy-start.113
  145.5 112.2 %all-gather.24.cloned.1.call-start = ((), (), s32[]{:S(2)}) async-start(), calls=%async_computation.18 | async-start | bytes 9830400 | tf_op jit(solution)/shard_map/all_gather | solution.py:172
  168.2 7.9 copy-start.7
  173.0 142.2 %all-gather.22.cloned.1.call-start = ((), (), s32[]{:S(2)}) async-start(), calls=%async_computation.17 | async-start | bytes 9830400 | tf_op jit(solution)/shard_map/all_gather | solution.py:172
  193.2 13.2 %copy-start.11 = (bf16[1280,3,64]{0,2,1:T(8,128)(2,1)}, bf16[1280,3,64]{0,2,1:T(8,128)(2,1)S(1)}, u32[]{:S(2)}) copy-start(bf16[1280,3,64]{0,2,1:T(8,128)(2,1)S(1)} %get-tuple-element.1332) | copy-start | bytes 1474564
  193.3 13.2 %copy-start.24 = (pred[2,640,1280]{2,1,0:T(8,128)(4,1)}, pred[2,640,1280]{2,1,0:T(8,128)(4,1)S(1)}, u32[]{:S(2)}) copy-start(pred[2,640,1280]{2,1,0:T(8,128)(4,1)S(1)} %get-tuple-element.1335) | copy-start | bytes 4915204
  193.3 13.2 %copy-start.117 = (f32[2,3,640,1]{2,1,3,0:T(4,128)}, f32[2,3,640,1]{2,1,3,0:T(4,128)S(1)}, u32[]{:S(2)}) copy-start(f32[2,3,640,1]{2,1,3,0:T(4,128)S(1)} %get-tuple-element.1185) | copy-start | bytes 46084
  193.9 12.6 %copy-start.68 = (bf16[24,8,2,640]{3,1,2,0:T(8,128)(2,1)}, bf16[24,8,2,640]{3,1,2,0:T(8,128)(2,1)S(1)}, u32[]{:S(2)}) copy-start(bf16[24,8,2,640]{3,1,2,0:T(8,128)(2,1)S(1)} %copy.102) | copy-start | bytes 1474564
  195.9 162.5 %all-gather.12.cloned.1.call-start = ((), (), s32[]{:S(2)}) async-start(), calls=%async_computation.6 | async-start | bytes 1327104 | tf_op jit(solution)/shard_map/all_gather | solution.py:141
  196.5 203.8 %all-gather.14.cloned.1.call-start = ((), (), s32[]{:S(2)}) async-start(), calls=%async_computation.7 | async-start | bytes 1327104 | tf_op jit(solution)/shard_map/all_gather | solution.py:142
  197.1 273.3 %reduce-scatter.7.cloned.1.call-start = ((), (), s32[]{:S(2)}) async-start(), calls=%async_computation.8 | async-start | bytes 2457600 | tf_op jit(solution)/shard_map/reduce_scatter | solution.py:200
  315.2 15.2 %slice-start = ((s8[5898240]{0:T(1024)(128)(4,1)}), s8[1703936]{0:T(1024)(128)(4,1)S(1)}, s32[]{:S(2)}) async-start(s8[5898240]{0:T(1024)(128)(4,1)} %bitcast.552), calls=%async_computation.22 | async-start | bytes 3407872
  321.7 8.7 slice-start.1
  321.7 8.7 copy-start.13
  321.7 9.8 copy-start.16
  321.7 10.4 copy-start.18
  336.1 22.3 %copy-start.145 = (f32[768]{0:T(1024)S(1)}, f32[768]{0:T(1024)}, u32[]{:S(2)}) copy-start(f32[768]{0:T(1024)} %param.41) | copy-start | bytes 9220
  336.1 22.3 %copy-start.175 = (f32[768]{0:T(1024)S(1)}, f32[768]{0:T(1024)}, u32[]{:S(2)}) copy-start(f32[768]{0:T(1024)} %param.36) | copy-start | bytes 9220
  336.1 22.3 %copy-start.176 = (f32[768]{0:T(1024)S(1)}, f32[768]{0:T(1024)}, u32[]{:S(2)}) copy-start(f32[768]{0:T(1024)} %param.42) | copy-start | bytes 9220
  358.4 41.9 %copy-start.147 = (f32[768]{0:T(1024)S(1)}, f32[768]{0:T(1024)}, u32[]{:S(2)}) copy-start(f32[768]{0:T(1024)} %param.44) | copy-start | bytes 9220
  400.2 9.0 copy-start.174
  412.3 62.2 %reduce-scatter.11.cloned.1.call-start = ((), (), s32[]{:S(2)}) async-start(), calls=%async_computation.11 | async-start | bytes 2457600 | tf_op jit(solution)/shard_map/reduce_scatter | solution.py:200
  412.3 12.1 %copy-start.173 = (bf16[768,768]{0,1:T(8,128)(2,1)S(1)}, bf16[768,768]{0,1:T(8,128)(2,1)}, u32[]{:S(2)}) copy-start(bf16[768,768]{0,1:T(8,128)(2,1)} %all-gather.14.cloned.1.call-done) | copy-start | bytes 3538948
  433.9 74.1 %reduce-scatter.15.cloned.1.call-start = ((), (), s32[]{:S(2)}) async-start(), calls=%async_computation.14 | async-start | bytes 2457600 | tf_op jit(solution)/shard_map/reduce_scatter | solution.py:200
  455.6 105.9 %all-gather.20.cloned.1.call-start = ((), (), s32[]{:S(2)}) async-start(), calls=%async_computation.15 | async-start | bytes 2457600 | tf_op jit(solution)/shard_map/all_gather | solution.py:221
  455.6 7.6 copy-start.19
  470.4 41.5 %copy-start.92 = (bf16[320,768]{1,0:T(8,128)(2,1)S(1)}, bf16[320,768]{1,0:T(8,128)(2,1)}, u32[]{:S(2)}) copy-start(bf16[320,768]{1,0:T(8,128)(2,1)} %reduce-scatter.7.cloned.1.call-done) | copy-start | bytes 1474564
  474.5 37.5 %copy-start.93 = (bf16[320,768]{1,0:T(8,128)(2,1)S(1)}, bf16[320,768]{1,0:T(8,128)(2,1)}, u32[]{:S(2)}) copy-start(bf16[320,768]{1,0:T(8,128)(2,1)} %reduce-scatter.11.cloned.1.call-done) | copy-start | bytes 1474564
  517.9 12.6 %slice-start.4 = ((s8[5898240]{0:T(1024)(128)(4,1)}), s8[1703936]{0:T(1024)(128)(4,1)S(1)}, s32[]{:S(2)}) async-start(s8[5898240]{0:T(1024)(128)(4,1)} %bitcast.562), calls=%async_computation.26 | async-start | bytes 3407872
  519.2 108.3 %all-gather.16.cloned.1.call-start = ((), (), s32[]{:S(2)}) async-start(), calls=%async_computation.9 | async-start | bytes 2457600 | tf_op jit(solution)/shard_map/all_gather | solution.py:221
  519.8 180.1 %all-gather.18.cloned.1.call-start = ((), (), s32[]{:S(2)}) async-start(), calls=%async_computation.12 | async-start | bytes 2457600 | tf_op jit(solution)/shard_map/all_gather | solution.py:221
  537.0 240.9 %all-reduce.9.cloned.1.call-start = ((), (), s32[]{:S(2)}) async-start(), calls=%async_computation.21 | async-start | bytes 11796480 | tf_op jit(solution)/shard_map/psum | solution.py:184
  561.2 8.9 copy-start.10
  561.2 8.9 copy-start.23
  561.2 8.9 copy-start.31
  561.2 8.9 copy-start.48
  561.2 8.9 copy-start.114
  561.2 273.0 %reduce-scatter.17.cloned.1.call-start = ((), (), s32[]{:S(2)}) async-start(), calls=%async_computation.16 | async-start | bytes 2457600 | tf_op jit(solution)/shard_map/reduce_scatter | solution.py:254
  627.5 7.1 copy-start.42
  640.1 195.9 %reduce-scatter.9.cloned.1.call-start = ((), (), s32[]{:S(2)}) async-start(), calls=%async_computation.10 | async-start | bytes 2457600 | tf_op jit(solution)/shard_map/reduce_scatter | solution.py:254
  710.6 128.8 %reduce-scatter.13.cloned.1.call-start = ((), (), s32[]{:S(2)}) async-start(), calls=%async_computation.13 | async-start | bytes 2457600 | tf_op jit(solution)/shard_map/reduce_scatter | solution.py:254
  743.1 7.2 copy-start.2
  772.1 12.8 %copy-start.79 = (bf16[1280,1,192]{0,2,1:T(8,128)(2,1)}, bf16[1280,1,192]{0,2,1:T(8,128)(2,1)S(1)}, u32[]{:S(2)}) copy-start(bf16[1280,1,192]{0,2,1:T(8,128)(2,1)S(1)} %stack_reshape.39) | copy-start | bytes 1474564
  773.6 11.4 %copy-start.77 = (bf16[1280,3,64]{0,2,1:T(8,128)(2,1)}, bf16[1280,3,64]{0,2,1:T(8,128)(2,1)S(1)}, u32[]{:S(2)}) copy-start(bf16[1280,3,64]{0,2,1:T(8,128)(2,1)S(1)} %convert.56) | copy-start | bytes 1474564
  777.6 269.1 %all-reduce.7.cloned.1.call-start = ((), (), s32[]{:S(2)}) async-start(), calls=%async_computation.20 | async-start | bytes 14155776 | tf_op jit(solution)/shard_map/psum | solution.py:273
  809.5 26.5 %copy-start.56 = (f32[320,768]{1,0:T(8,128)S(1)}, f32[320,768]{1,0:T(8,128)}, u32[]{:S(2)}) copy-start(f32[320,768]{1,0:T(8,128)} %copy-done.55) | copy-start | bytes 2949124
  809.5 26.5 %copy-start.163 = (f32[320]{0:T(512)S(1)}, f32[320]{0:T(512)}, u32[]{:S(2)}) copy-start(f32[320]{0:T(512)} %dynamic-slice.26) | copy-start | bytes 3844
  810.0 29.4 %copy-start.54 = (f32[320,768]{1,0:T(8,128)S(1)}, f32[320,768]{1,0:T(8,128)}, u32[]{:S(2)}) copy-start(f32[320,768]{1,0:T(8,128)} %copy-done.53) | copy-start | bytes 2949124
  810.0 29.4 %copy-start.162 = (f32[320]{0:T(512)S(1)}, f32[320]{0:T(512)}, u32[]{:S(2)}) copy-start(f32[320]{0:T(512)} %dynamic-slice.22) | copy-start | bytes 3844
  836.0 48.8 %copy-start.58 = (f32[320,768]{1,0:T(8,128)S(1)}, f32[320,768]{1,0:T(8,128)}, u32[]{:S(2)}) copy-start(f32[320,768]{1,0:T(8,128)} %copy-done.57) | copy-start | bytes 2949124
  836.0 48.8 %copy-start.165 = (f32[320]{0:T(512)S(1)}, f32[320]{0:T(512)}, u32[]{:S(2)}) copy-start(f32[320]{0:T(512)} %dynamic-slice.24) | copy-start | bytes 3844
  839.3 47.0 %copy-start.95 = (bf16[1,320,768]{2,1,0:T(8,128)(2,1)S(1)}, bf16[1,320,768]{2,1,0:T(8,128)(2,1)}, u32[]{:S(2)}) copy-start(bf16[1,320,768]{2,1,0:T(8,128)(2,1)} %get-tuple-element.736) | copy-start | bytes 1474564
  839.4 45.5 %copy-start.89 = (bf16[320,768]{1,0:T(8,128)(2,1)S(1)}, bf16[320,768]{1,0:T(8,128)(2,1)}, u32[]{:S(2)}) copy-start(bf16[320,768]{1,0:T(8,128)(2,1)} %reduce-scatter.13.cloned.1.call-done) | copy-start | bytes 1474564
  (174 other events, 600.0 us)
Sparse Core Ops, SparseCore 0:
  145.6 54.5 all-gather.25
  202.4 55.2 all-gather.23
  259.9 55.2 all-gather.21
  317.2 41.1 all-gather.11
  360.4 39.8 all-gather.13
  412.4 29.0 reduce-scatter.6
  444.1 30.3 reduce-scatter.10
  477.6 30.3 reduce-scatter.14
  519.3 21.8 all-gather.19
  542.6 21.8 all-gather.15
  566.0 21.8 all-gather.17
  590.3 113.2 all-reduce.8
  706.2 30.5 reduce-scatter.16
  739.2 30.3 reduce-scatter.8
  777.7 30.4 reduce-scatter.12
  813.7 232.9 all-reduce.6
